TPU v7x, 128 devices: a whole 4x4x4 slice. The times are simulated.
128 devices in a mesh: blk: 128 (over y, z, x, core).
Axes of the slice: x: 4, y: 4, z: 4, core: 2. Of those that a mesh axis runs over, the one named last changes fastest.
Arguments:
- defect: float32 [1536, 128], P('blk'), may hold values from -6 to 6
- mass: float32 [1536, 128], P('blk'), may hold values from 1 to 2
- block_diag: float32 [1536, 128, 128], P('blk'), may hold values from -0.1875 to 0.1875
- coupling: float32 [12288, 128, 128], P('blk'), may hold values from -0.09375 to 0.09375
- tile_rows: int32 [12288], P('blk'), may hold values from 0 to 1535, as said below
- tile_cols: int32 [12288], P('blk'), may hold values from 0 to 1535, as said below
Outputs:
- update: float32 [1536, 128], P('blk')
Inputs may be any that keep to these rules, and one draw needn't show every extreme that they name: `tile_rows`: block rows d * 12 to d * 12 + 11 belong to device d of blk, and each device holds the tiles at positions d * 96 to d * 96 + 95. Of every tile a device holds, exactly one of its block row and block column belongs to that device; the other belongs to a different device. Exactly half of the 96 tiles of every device have their block row with that device, and the other half their block column. A program may send only the blocks and products of tiles that exist; slots of a padded buffer that no tile fills need not be sent. `tile_cols`: of one device's tiles, at most 1 have their block column with any one other device and at most 1 have their block row with any one other device; every device reaches 1 with some other device on each of the two sides.
All inputs are finite; a program needn't handle non-finite values.
Results may differ from a plain program's by a relative error of at most 0.0001.
Values sent between devices are 32-bit elements; how exact they have to be, the bound alone decides.
A program may use at most 64 MiB of HBM per device.

v0:
```python
import functools

import jax
import jax.numpy as jnp
from jax import lax
from jax.sharding import Mesh
from jax.sharding import PartitionSpec as P

ITERS = 3
BLK = ("blk_0", "blk_1", "blk_2", "blk_3")


def side_by_side(arrays, axis, split_dim, concat_dim, along):
    both = jnp.concatenate(arrays, axis=along)
    out, at, gathered = (
        lax.all_to_all(both, axis, split_axis=split_dim, concat_axis=concat_dim, tiled=True),
        0,
        [],
    )
    for a in arrays:
        gathered.append(lax.slice_in_dim(out, at, at + a.shape[along], axis=along))
        at += a.shape[along]
    return tuple(gathered)


def one_axis_at_a_time(x, axes):
    return functools.reduce(lax.psum, axes, x)


def solve_small(gram, target):
    factor = jnp.linalg.cholesky(gram)
    count = gram.shape[0]
    forward = []
    for index in range(count):
        value = target[index]
        for inner in range(index):
            value = value - factor[index, inner] * forward[inner]
        forward.append(value / factor[index, index])
    backward = [None] * count
    for index in reversed(range(count)):
        value = forward[index]
        for inner in range(index + 1, count):
            value = value - factor[inner, index] * backward[inner]
        backward[index] = value / factor[index, index]
    return backward


def tile_products(coupling, inputs):
    return jnp.einsum("tij,tj->ti", coupling, inputs, precision=lax.Precision.HIGHEST)


def row_sum(targets, values, rows_here):
    onehot = (jnp.arange(rows_here, dtype=jnp.int32)[:, None] == targets[None, :]).astype(
        jnp.float32
    )
    return jnp.dot(
        onehot, values, precision=lax.Precision.HIGHEST, preferred_element_type=jnp.float32
    )


def lane_slots(lanes, lane_count):
    onehot = (lanes[:, None] == jnp.arange(lane_count, dtype=jnp.int32)[None, :]).astype(jnp.int32)
    before = jnp.cumsum(onehot, axis=0) - onehot
    return jnp.sum(before * onehot, axis=1)


def on_device(defect, mass, block_diag, coupling, tile_rows, tile_cols):
    rows_here = defect.shape[0]
    width = defect.shape[1]
    tiles_here = tile_rows.shape[0]
    devices = lax.axis_size(BLK)
    slots = (tiles_here // 2 + devices - 2) // (devices - 1)
    myself = lax.axis_index(BLK)
    row_owner = tile_rows // rows_here
    col_owner = tile_cols // rows_here
    row_local = tile_rows % rows_here
    col_local = tile_cols % rows_here
    fetch_need = col_owner != myself
    push_need = row_owner != myself
    fetch_lane = jnp.where(fetch_need, col_owner, devices)
    push_lane = jnp.where(push_need, row_owner, devices)
    fetch_slot = lane_slots(fetch_lane, devices)
    push_slot = lane_slots(push_lane, devices)
    requests = (
        jnp.zeros((devices, slots), jnp.int32)
        .at[fetch_lane, fetch_slot]
        .set(col_local, mode="drop")
    )
    targets = (
        jnp.zeros((devices, slots), jnp.int32).at[push_lane, push_slot].set(row_local, mode="drop")
    )
    asked, landing = side_by_side((requests, targets), BLK, 0, 0, 1)
    fetch_pick = jnp.minimum(fetch_lane, devices - 1)
    kept_rows = jnp.where(push_need, -1, row_local)
    landing_flat = landing.reshape(-1)
    negated = -defect
    beta = jnp.sqrt(one_axis_at_a_time(jnp.sum(negated * negated), BLK))
    basis = [negated / beta]
    upper = jnp.zeros((ITERS + 1, ITERS), jnp.float32)
    for column in range(ITERS):
        apply_vector = basis[column]
        fetched = lax.all_to_all(apply_vector[asked], BLK, split_axis=0, concat_axis=0, tiled=True)
        inputs = jnp.where(
            fetch_need[:, None], fetched[fetch_pick, fetch_slot], apply_vector[col_local]
        )
        products = tile_products(coupling, inputs)
        outgoing = (
            jnp.zeros((devices, slots, width), jnp.float32)
            .at[push_lane, push_slot]
            .set(products, mode="drop")
        )
        arrived = lax.all_to_all(outgoing, BLK, split_axis=0, concat_axis=0, tiled=True)
        local_rows = row_sum(kept_rows, products, rows_here)
        remote_rows = row_sum(landing_flat, arrived.reshape(-1, width), rows_here)
        own = jnp.einsum("rij,rj->ri", block_diag, apply_vector, precision=lax.Precision.HIGHEST)
        image = mass * apply_vector + own + local_rows + remote_rows
        local_dots = jnp.stack([jnp.sum(item * image) for item in basis])
        dots, square = (
            one_axis_at_a_time(local_dots, BLK),
            one_axis_at_a_time(jnp.sum(image * image), BLK),
        )
        for index in range(column + 1):
            image = image - dots[index] * basis[index]
        norm = jnp.sqrt(square - jnp.sum(dots * dots))
        upper = upper.at[: column + 1, column].set(dots)
        upper = upper.at[column + 1, column].set(norm)
        if column + 1 < ITERS:
            basis.append(image / norm)
    gram = jnp.dot(
        upper.T, upper, precision=lax.Precision.HIGHEST, preferred_element_type=jnp.float32
    )
    mixing = solve_small(gram, beta * upper[0, :])
    update = jnp.zeros_like(defect)
    for index in range(ITERS):
        update = update + mixing[index] * basis[index]
    return update


def solution(mesh):
    split = Mesh(mesh.devices.reshape(4, 4, 4, 2), ("blk_0", "blk_1", "blk_2", "blk_3"))
    return jax.shard_map(
        on_device,
        mesh=split,
        in_specs=(
            P(BLK, None),
            P(BLK, None),
            P(BLK, None, None),
            P(BLK, None, None),
            P(BLK),
            P(BLK),
        ),
        out_specs=P(BLK, None),
        check_vma=False,
    )
```

profile of v0, /device:TPU:1, one launch (start us, length us, event | category | flops | bytes accessed | tf_op | source)
XLA Modules:
  0.0 318.7 jit_solution(14043822373592717138)
XLA Ops:
  0.0 1.4 multiply_reduce_fusion.9
  1.4 10.1 %psum.196 = f32[]{:T(128)} all-reduce(f32[]{:T(128)} %multiply_reduce_fusion.9), channel_id=1, replica_groups=mesh['blk_0'=4,'blk_1'=4,'blk_2'=4,'blk_3'=2] {'blk_0'}, use_global_device_ids=true, to_apply=%region_1.2 | all-reduce | flops 1 | bytes 8 | tf_op jit(solution)/shard_map/psum | solution.py:27
  11.5 10.4 %psum.197 = f32[]{:T(128)} all-reduce(f32[]{:T(128)} %psum.196), channel_id=1, replica_groups=mesh['blk_0'=4,'blk_1'=4,'blk_2'=4,'blk_3'=2] {'blk_1'}, use_global_device_ids=true, to_apply=%region_2.3 | all-reduce | flops 1 | bytes 8 | tf_op jit(solution)/shard_map/psum | solution.py:27
  21.9 9.1 %psum.198 = f32[]{:T(128)} all-reduce(f32[]{:T(128)} %psum.197), channel_id=1, replica_groups=mesh['blk_0'=4,'blk_1'=4,'blk_2'=4,'blk_3'=2] {'blk_2'}, use_global_device_ids=true, to_apply=%region_3.4 | all-reduce | flops 1 | bytes 8 | tf_op jit(solution)/shard_map/psum | solution.py:27
  33.8 0.9 scatter_custom_fusion.1
  34.7 0.9 scatter_custom_fusion
  35.6 0.7 copy.18
  36.3 10.1 %all-to-all-start = ((s32[128,1,2]{2,1,0:T(1,128)}), s32[128,1,2]{2,1,0:T(1,128)S(1)}, u32[]{:S(2)}, u32[]{:S(2)}) async-start(s32[128,1,2]{2,1,0:T(1,128)} %copy.18), calls=%async_computation | async-start | bytes 131072 | tf_op jit(solution)/shard_map/all_to_all | solution.py:16
  46.5 4.0 %psum.199 = f32[]{:T(128)} all-reduce(f32[]{:T(128)} %psum.198), channel_id=1, replica_groups=mesh['blk_0'=4,'blk_1'=4,'blk_2'=4,'blk_3'=2] {'blk_3'}, use_global_device_ids=true, to_apply=%region_4.5 | all-reduce | flops 1 | bytes 8 | tf_op jit(solution)/shard_map/psum | solution.py:27
  51.1 0.7 negate_divide_fusion
  51.9 0.7 fusion.61
  53.2 1.3 and_reduce_fusion
  54.6 1.3 fusion.13
  55.9 0.7 compare_reduce_fusion.1
  57.4 1.2 gather_fusion
  58.7 9.0 %all-to-all-start.1 = ((f32[128,1,128]{2,1,0:T(1,128)}), f32[128,1,128]{2,1,0:T(1,128)S(1)}, u32[]{:S(2)}, u32[]{:S(2)}) async-start(f32[128,1,128]{2,1,0:T(1,128)} %bitcast.13), calls=%async_computation.1 | async-start | bytes 131072 | tf_op jit(solution)/shard_map/all_to_all | solution.py:102
  68.3 8.9 %all-to-all-done.1 = f32[128,1,128]{2,1,0:T(1,128)S(1)} async-done(((f32[128,1,128]{2,1,0:T(1,128)}), f32[128,1,128]{2,1,0:T(1,128)S(1)}, u32[]{:S(2)}, u32[]{:S(2)}) %all-to-all-start.1) | async-done | bytes 65568 | tf_op jit(solution)/shard_map/all_to_all | solution.py:102
  77.2 0.8 gather_fusion.1
  78.2 11.8 %fusion.40 = f32[96,1,128]{2,1,0:T(1,128)S(1)} fusion(f32[96,128,1]{1,2,0:T(1,128)S(1)} %bitcast.152, f32[96,128,128]{2,1,0:T(8,128)} %param.21), kind=kOutput, calls=%fused_computation.123 | convolution fusion | flops 18874368 | bytes 6389760 | tf_op jit(solution)/shard_map/tij,tj->ti/dot_general | solution.py:49
  90.0 1.4 scatter_custom_fusion.2
  91.4 4.6 %all-to-all-start.2 = ((f32[128,1,128]{2,1,0:T(1,128)}), f32[128,1,128]{2,1,0:T(1,128)S(1)}, u32[]{:S(2)}, u32[]{:S(2)}) async-start(f32[128,1,128]{2,1,0:T(1,128)} %bitcast.20), calls=%async_computation.2 | async-start | bytes 131072 | tf_op jit(solution)/shard_map/all_to_all | solution.py:112
  96.1 9.4 %all-to-all-done.2 = f32[128,1,128]{2,1,0:T(1,128)S(1)} async-done(((f32[128,1,128]{2,1,0:T(1,128)}), f32[128,1,128]{2,1,0:T(1,128)S(1)}, u32[]{:S(2)}, u32[]{:S(2)}) %all-to-all-start.2) | async-done | bytes 65568 | tf_op jit(solution)/shard_map/all_to_all | solution.py:112
  105.5 0.8 multiply_reduce_fusion.8
  106.3 7.5 %all-reduce.9 = (f32[]{:T(128)}, f32[1]{0:T(128)}) all-reduce(f32[]{:T(128)} %get-tuple-element.87, f32[1]{0:T(128)} %bitcast.22), channel_id=1, replica_groups=mesh['blk_0'=4,'blk_1'=4,'blk_2'=4,'blk_3'=2] {'blk_0'}, use_global_device_ids=true, to_apply=%region_18.19 | all-reduce | flops 2 | bytes 16 | tf_op jit(solution)/shard_map/psum | solution.py:27
  113.8 7.4 %all-reduce.6 = (f32[]{:T(128)}, f32[1]{0:T(128)}) all-reduce(f32[]{:T(128)} %get-tuple-element.104, f32[1]{0:T(128)} %get-tuple-element.105), channel_id=1, replica_groups=mesh['blk_0'=4,'blk_1'=4,'blk_2'=4,'blk_3'=2] {'blk_1'}, use_global_device_ids=true, to_apply=%region_19.20 | all-reduce | flops 2 | bytes 16 | tf_op jit(solution)/shard_map/psum | solution.py:27
  121.2 7.6 %all-reduce.3 = (f32[]{:T(128)}, f32[1]{0:T(128)}) all-reduce(f32[]{:T(128)} %get-tuple-element.98, f32[1]{0:T(128)} %get-tuple-element.99), channel_id=1, replica_groups=mesh['blk_0'=4,'blk_1'=4,'blk_2'=4,'blk_3'=2] {'blk_2'}, use_global_device_ids=true, to_apply=%region_20.21 | all-reduce | flops 2 | bytes 16 | tf_op jit(solution)/shard_map/psum | solution.py:27
  128.7 9.4 %all-reduce.12 = (f32[]{:T(128)}, f32[1]{0:T(128)}) all-reduce(f32[]{:T(128)} %get-tuple-element.92, f32[1]{0:T(128)} %get-tuple-element.93), channel_id=1, replica_groups=mesh['blk_0'=4,'blk_1'=4,'blk_2'=4,'blk_3'=2] {'blk_3'}, use_global_device_ids=true, to_apply=%region_21.22 | all-reduce | flops 2 | bytes 16 | tf_op jit(solution)/shard_map/psum | solution.py:27
  140.7 1.2 gather_fusion.3
  142.0 3.7 %all-to-all-start.3 = ((f32[128,1,128]{2,1,0:T(1,128)}), f32[128,1,128]{2,1,0:T(1,128)S(1)}, u32[]{:S(2)}, u32[]{:S(2)}) async-start(f32[128,1,128]{2,1,0:T(1,128)} %bitcast.30), calls=%async_computation.3 | async-start | bytes 131072 | tf_op jit(solution)/shard_map/all_to_all | solution.py:102
  145.7 1.3 fusion.11
  148.6 6.7 %all-to-all-done.3 = f32[128,1,128]{2,1,0:T(1,128)S(1)} async-done(((f32[128,1,128]{2,1,0:T(1,128)}), f32[128,1,128]{2,1,0:T(1,128)S(1)}, u32[]{:S(2)}, u32[]{:S(2)}) %all-to-all-start.3) | async-done | bytes 65568 | tf_op jit(solution)/shard_map/all_to_all | solution.py:102
  155.4 0.8 gather_fusion.4
  156.3 11.8 %fusion.41 = f32[96,1,128]{2,1,0:T(1,128)S(1)} fusion(f32[96,128,1]{1,2,0:T(1,128)S(1)} %bitcast.153, f32[96,128,128]{2,1,0:T(8,128)} %param.21), kind=kOutput, calls=%fused_computation.124 | convolution fusion | flops 18874368 | bytes 6389760 | tf_op jit(solution)/shard_map/tij,tj->ti/dot_general | solution.py:49
  168.1 1.4 scatter_custom_fusion.3
  169.5 4.6 %all-to-all-start.4 = ((f32[128,1,128]{2,1,0:T(1,128)}), f32[128,1,128]{2,1,0:T(1,128)S(1)}, u32[]{:S(2)}, u32[]{:S(2)}) async-start(f32[128,1,128]{2,1,0:T(1,128)} %bitcast.36), calls=%async_computation.4 | async-start | bytes 131072 | tf_op jit(solution)/shard_map/all_to_all | solution.py:112
  174.3 9.4 %all-to-all-done.4 = f32[128,1,128]{2,1,0:T(1,128)S(1)} async-done(((f32[128,1,128]{2,1,0:T(1,128)}), f32[128,1,128]{2,1,0:T(1,128)S(1)}, u32[]{:S(2)}, u32[]{:S(2)}) %all-to-all-start.4) | async-done | bytes 65568 | tf_op jit(solution)/shard_map/all_to_all | solution.py:112
  183.7 0.8 multiply_reduce_fusion.6
  184.5 1.3 pad_maximum_fusion
  185.8 7.4 %all-reduce.8 = (f32[]{:T(128)}, f32[2]{0:T(128)S(1)}) all-reduce(f32[]{:T(128)} %get-tuple-element.84, f32[2]{0:T(128)S(1)} %pad_maximum_fusion), channel_id=1, replica_groups=mesh['blk_0'=4,'blk_1'=4,'blk_2'=4,'blk_3'=2] {'blk_0'}, use_global_device_ids=true, to_apply=%region_31.32 | all-reduce | flops 3 | bytes 24 | tf_op jit(solution)/shard_map/psum | solution.py:27
  193.2 7.4 %all-reduce.5 = (f32[]{:T(128)}, f32[2]{0:T(128)S(1)}) all-reduce(f32[]{:T(128)} %get-tuple-element.102, f32[2]{0:T(128)S(1)} %get-tuple-element.103), channel_id=1, replica_groups=mesh['blk_0'=4,'blk_1'=4,'blk_2'=4,'blk_3'=2] {'blk_1'}, use_global_device_ids=true, to_apply=%region_32.33 | all-reduce | flops 3 | bytes 24 | tf_op jit(solution)/shard_map/psum | solution.py:27
  200.6 7.5 %all-reduce.2 = (f32[]{:T(128)}, f32[2]{0:T(128)S(1)}) all-reduce(f32[]{:T(128)} %get-tuple-element.96, f32[2]{0:T(128)S(1)} %get-tuple-element.97), channel_id=1, replica_groups=mesh['blk_0'=4,'blk_1'=4,'blk_2'=4,'blk_3'=2] {'blk_2'}, use_global_device_ids=true, to_apply=%region_33.34 | all-reduce | flops 3 | bytes 24 | tf_op jit(solution)/shard_map/psum | solution.py:27
  208.1 9.4 %all-reduce.11 = (f32[]{:T(128)}, f32[2]{0:T(128)S(1)}) all-reduce(f32[]{:T(128)} %get-tuple-element.90, f32[2]{0:T(128)S(1)} %get-tuple-element.91), channel_id=1, replica_groups=mesh['blk_0'=4,'blk_1'=4,'blk_2'=4,'blk_3'=2] {'blk_3'}, use_global_device_ids=true, to_apply=%region_34.35 | all-reduce | flops 3 | bytes 24 | tf_op jit(solution)/shard_map/psum | solution.py:27
  220.2 1.2 subtract_divide_fusion
  221.4 1.2 gather_fusion.6
  222.6 3.7 %all-to-all-start.5 = ((f32[128,1,128]{2,1,0:T(1,128)}), f32[128,1,128]{2,1,0:T(1,128)S(1)}, u32[]{:S(2)}, u32[]{:S(2)}) async-start(f32[128,1,128]{2,1,0:T(1,128)} %bitcast.49), calls=%async_computation.5 | async-start | bytes 131072 | tf_op jit(solution)/shard_map/all_to_all | solution.py:102
  226.4 1.3 fusion.9
  227.7 2.0 broadcast_select_fusion.4
  230.3 1.4 scatter.71
  231.9 4.2 %all-to-all-done.5 = f32[128,1,128]{2,1,0:T(1,128)S(1)} async-done(((f32[128,1,128]{2,1,0:T(1,128)}), f32[128,1,128]{2,1,0:T(1,128)S(1)}, u32[]{:S(2)}, u32[]{:S(2)}) %all-to-all-start.5) | async-done | bytes 65568 | tf_op jit(solution)/shard_map/all_to_all | solution.py:102
  236.0 0.8 gather_fusion.7
  236.9 11.8 %fusion.42 = f32[96,1,128]{2,1,0:T(1,128)S(1)} fusion(f32[96,128,1]{1,2,0:T(1,128)S(1)} %bitcast.151, f32[96,128,128]{2,1,0:T(8,128)} %param.21), kind=kOutput, calls=%fused_computation.125 | convolution fusion | flops 18874368 | bytes 6389760 | tf_op jit(solution)/shard_map/tij,tj->ti/dot_general | solution.py:49
  248.8 1.4 scatter_custom_fusion.4
  250.2 5.7 %all-to-all-start.6 = ((f32[128,1,128]{2,1,0:T(1,128)}), f32[128,1,128]{2,1,0:T(1,128)S(1)}, u32[]{:S(2)}, u32[]{:S(2)}) async-start(f32[128,1,128]{2,1,0:T(1,128)} %bitcast.55), calls=%async_computation.6 | async-start | bytes 131072 | tf_op jit(solution)/shard_map/all_to_all | solution.py:112
  256.1 9.4 %all-to-all-done.6 = f32[128,1,128]{2,1,0:T(1,128)S(1)} async-done(((f32[128,1,128]{2,1,0:T(1,128)}), f32[128,1,128]{2,1,0:T(1,128)S(1)}, u32[]{:S(2)}, u32[]{:S(2)}) %all-to-all-start.6) | async-done | bytes 65568 | tf_op jit(solution)/shard_map/all_to_all | solution.py:112
  265.5 0.8 multiply_reduce_fusion
  266.3 2.0 pad_maximum_fusion.1
  268.3 7.4 %all-reduce.7 = (f32[3]{0:T(128)S(1)}, f32[]{:T(128)}) all-reduce(f32[3]{0:T(128)S(1)} %pad_maximum_fusion.1, f32[]{:T(128)} %get-tuple-element.79), channel_id=1, replica_groups=mesh['blk_0'=4,'blk_1'=4,'blk_2'=4,'blk_3'=2] {'blk_0'}, use_global_device_ids=true, to_apply=%region_41.42 | all-reduce | flops 4 | bytes 32 | tf_op jit(solution)/shard_map/psum | solution.py:27
  275.7 7.4 %all-reduce.4 = (f32[3]{0:T(128)S(1)}, f32[]{:T(128)}) all-reduce(f32[3]{0:T(128)S(1)} %get-tuple-element.100, f32[]{:T(128)} %get-tuple-element.101), channel_id=1, replica_groups=mesh['blk_0'=4,'blk_1'=4,'blk_2'=4,'blk_3'=2] {'blk_1'}, use_global_device_ids=true, to_apply=%region_42.43 | all-reduce | flops 4 | bytes 32 | tf_op jit(solution)/shard_map/psum | solution.py:27
  283.1 7.5 %all-reduce.1 = (f32[3]{0:T(128)S(1)}, f32[]{:T(128)}) all-reduce(f32[3]{0:T(128)S(1)} %get-tuple-element.94, f32[]{:T(128)} %get-tuple-element.95), channel_id=1, replica_groups=mesh['blk_0'=4,'blk_1'=4,'blk_2'=4,'blk_3'=2] {'blk_2'}, use_global_device_ids=true, to_apply=%region_43.44 | all-reduce | flops 4 | bytes 32 | tf_op jit(solution)/shard_map/psum | solution.py:27
  290.6 9.4 %all-reduce.10 = (f32[3]{0:T(128)S(1)}, f32[]{:T(128)}) all-reduce(f32[3]{0:T(128)S(1)} %get-tuple-element.88, f32[]{:T(128)} %get-tuple-element.89), channel_id=1, replica_groups=mesh['blk_0'=4,'blk_1'=4,'blk_2'=4,'blk_3'=2] {'blk_3'}, use_global_device_ids=true, to_apply=%region_44.45 | all-reduce | flops 4 | bytes 32 | tf_op jit(solution)/shard_map/psum | solution.py:27
  300.0 0.7 multiply_reduce_fusion.10
  300.7 1.9 broadcast_select_fusion.3
  302.5 1.3 scatter.74
  307.8 0.7 fusion.35
  (53 shorter events, 13.0 us)
Async XLA Ops:
  0.0 54.6 %copy-start = (f32[12,128,128]{2,1,0:T(8,128)S(1)}, f32[12,128,128]{2,1,0:T(8,128)}, u32[]{:S(2)}) copy-start(f32[12,128,128]{2,1,0:T(8,128)} %param.20) | copy-start | bytes 2359300
  0.0 140.1 %copy-start.1 = (f32[12,128]{1,0:T(8,128)S(1)}, f32[12,128]{1,0:T(8,128)}, u32[]{:S(2)}) copy-start(f32[12,128]{1,0:T(8,128)} %param.18) | copy-start | bytes 18436
  0.0 96.0 %copy-start.2 = (f32[12,128]{1,0:T(8,128)S(1)}, f32[12,128]{1,0:T(8,128)}, u32[]{:S(2)}) copy-start(f32[12,128]{1,0:T(8,128)} %param.19) | copy-start | bytes 18436
  36.3 20.9 %all-to-all-start = ((s32[128,1,2]{2,1,0:T(1,128)}), s32[128,1,2]{2,1,0:T(1,128)S(1)}, u32[]{:S(2)}, u32[]{:S(2)}) async-start(s32[128,1,2]{2,1,0:T(1,128)} %copy.18), calls=%async_computation | async-start | bytes 131072 | tf_op jit(solution)/shard_map/all_to_all | solution.py:16
  58.7 18.6 %all-to-all-start.1 = ((f32[128,1,128]{2,1,0:T(1,128)}), f32[128,1,128]{2,1,0:T(1,128)S(1)}, u32[]{:S(2)}, u32[]{:S(2)}) async-start(f32[128,1,128]{2,1,0:T(1,128)} %bitcast.13), calls=%async_computation.1 | async-start | bytes 131072 | tf_op jit(solution)/shard_map/all_to_all | solution.py:102
  91.4 14.1 %all-to-all-start.2 = ((f32[128,1,128]{2,1,0:T(1,128)}), f32[128,1,128]{2,1,0:T(1,128)S(1)}, u32[]{:S(2)}, u32[]{:S(2)}) async-start(f32[128,1,128]{2,1,0:T(1,128)} %bitcast.20), calls=%async_computation.2 | async-start | bytes 131072 | tf_op jit(solution)/shard_map/all_to_all | solution.py:112
  142.0 13.4 %all-to-all-start.3 = ((f32[128,1,128]{2,1,0:T(1,128)}), f32[128,1,128]{2,1,0:T(1,128)S(1)}, u32[]{:S(2)}, u32[]{:S(2)}) async-start(f32[128,1,128]{2,1,0:T(1,128)} %bitcast.30), calls=%async_computation.3 | async-start | bytes 131072 | tf_op jit(solution)/shard_map/all_to_all | solution.py:102
  169.5 14.1 %all-to-all-start.4 = ((f32[128,1,128]{2,1,0:T(1,128)}), f32[128,1,128]{2,1,0:T(1,128)S(1)}, u32[]{:S(2)}, u32[]{:S(2)}) async-start(f32[128,1,128]{2,1,0:T(1,128)} %bitcast.36), calls=%async_computation.4 | async-start | bytes 131072 | tf_op jit(solution)/shard_map/all_to_all | solution.py:112
  222.6 13.4 %all-to-all-start.5 = ((f32[128,1,128]{2,1,0:T(1,128)}), f32[128,1,128]{2,1,0:T(1,128)S(1)}, u32[]{:S(2)}, u32[]{:S(2)}) async-start(f32[128,1,128]{2,1,0:T(1,128)} %bitcast.49), calls=%async_computation.5 | async-start | bytes 131072 | tf_op jit(solution)/shard_map/all_to_all | solution.py:102
  250.2 15.3 %all-to-all-start.6 = ((f32[128,1,128]{2,1,0:T(1,128)}), f32[128,1,128]{2,1,0:T(1,128)S(1)}, u32[]{:S(2)}, u32[]{:S(2)}) async-start(f32[128,1,128]{2,1,0:T(1,128)} %bitcast.55), calls=%async_computation.6 | async-start | bytes 131072 | tf_op jit(solution)/shard_map/all_to_all | solution.py:112
where the time goes:
time: 320 us; the launch traced here: 319 us
  blocking collectives  129 us (40%)
  waiting for transfers between devices  48 us (15%)
  matrix products  42.5 us (13%)
  starting transfers between devices  41.6 us (13%)
  local copies, waits for them, and re-layouts  21.8 us (7%)
  other arithmetic  20.6 us (6%)
  between operations  15.3 us (5%)
    psum x16, blocking collectives, one_axis_at_a_time(): return functools.reduce(lax.psum, axes, x)  129 us
    dot_general x3, matrix products, tile_products(): jnp.einsum('tij,tj->ti', coupling, inputs, precision=lax.Precision.HIGHEST)  35.5 us
    all_to_all x3, waiting for transfers between devices, on_device(): lax.all_to_all(outgoing, BLK, split_axis=0, concat_axis=0, tiled=True)  28.2 us
    all_to_all x3, waiting for transfers between devices, on_device(): lax.all_to_all(apply_vector[asked], BLK, split_axis=0, concat_axis=0, til...  19.8 us
    all_to_all x3, starting transfers between devices, on_device(): lax.all_to_all(apply_vector[asked], BLK, split_axis=0, concat_axis=0, til...  16.5 us
    all_to_all x3, starting transfers between devices, on_device(): lax.all_to_all(outgoing, BLK, split_axis=0, concat_axis=0, tiled=True)  14.9 us
    all_to_all x1, starting transfers between devices, side_by_side(): lax.all_to_all(both, axis, split_axis=split_dim, concat_axis=concat_dim,...  10.1 us
  transfers between devices with their start and end apart: 7, of which 6 were waited for; matrix products, arithmetic and copies ran while one was open for 5% of the time, Pallas kernels for 0%

commit v1 on v0

v1 whole, which is shorter than its diff:
```python
import itertools

import jax
import jax.numpy as jnp
from jax import lax
from jax.experimental import pallas as pl
from jax.experimental.pallas import tpu as pltpu
from jax.sharding import PartitionSpec as P

N = 128
RB = 12
TD = 96
HALF = 48
B = 128
SHIFT = 1.5
F32 = jnp.float32
BF16 = jnp.bfloat16
MESH = pl.DeviceIdType.MESH


def distance(offset):
    return sum(min(step, 4 - step) for step in offset[:3]) + 0.5 * offset[3]


OFFSETS = sorted(
    (o for o in itertools.product(range(4), range(4), range(4), range(2)) if any(o)),
    key=distance,
    reverse=True,
)


def dot(a, b):
    return lax.dot_general(a, b, (((1,), (0,)), ((), ())), preferred_element_type=F32)


def dot_nt(a, b):
    return lax.dot_general(a, b, (((1,), (1,)), ((), ())), preferred_element_type=F32)


def iota(shape, dim):
    return lax.broadcasted_iota(jnp.int32, shape, dim)


def halves(x):
    high = x.astype(BF16)
    low = (x - high.astype(F32)).astype(BF16)
    return high, low


def total(x):
    return jnp.sum(jnp.sum(x, axis=0, keepdims=True), axis=1, keepdims=True)


def divided_by_rb(x):
    return lax.shift_right_logical(x * 21846, 18)


def kernel(
    defect_ref, mass_ref, diag_hbm, coup_hbm, rows_ref, cols_ref, out_ref,
    raw, raw_diag, weights, index_rows, perm_vmem, perm_smem,
    ysplit, products, oh_fetch_out, oh_push_in, oh_cols, oh_push_out, oh_local, oh_fetch_in,
    req_out, req_in, x_out, x_in, p_out, p_in, f_out, f_in,
    load_sem, perm_sem, send_sem, recv_sem,
):
    me = lax.axis_index("blk")
    y, z, x, c = me // 32, (me // 8) % 4, (me // 2) % 4, me % 2
    y_part = [((y + d) % 4) * 32 for d in range(4)]
    z_part = [((z + d) % 4) * 8 for d in range(4)]
    x_part = [((x + d) % 4) * 2 for d in range(4)]
    c_part = [(c + d) % 2 for d in range(2)]
    yz = [[y_part[a] + z_part[b] for b in range(4)] for a in range(4)]
    xc = [[x_part[a] + c_part[b] for b in range(2)] for a in range(4)]
    peers = [yz[o[0]][o[1]] + xc[o[2]][o[3]] for o in OFFSETS]

    req_in[...] = jnp.zeros_like(req_in)
    x_in[...] = jnp.zeros_like(x_in)
    p_in[...] = jnp.zeros_like(p_in)
    f_in[...] = jnp.zeros_like(f_in)

    barrier = pltpu.get_barrier_semaphore()
    for peer in peers:
        pl.semaphore_signal(barrier, inc=1, device_id=(peer,), device_id_type=MESH)

    loads = [
        pltpu.make_async_copy(
            coup_hbm.at[pl.ds(16 * i, 16)], raw.at[pl.ds(16 * i, 16)], load_sem.at[i]
        )
        for i in range(6)
    ]
    loads.append(pltpu.make_async_copy(diag_hbm, raw_diag, load_sem.at[6]))
    for load in loads:
        load.start()

    lane_row = iota((1, B), 1)
    lanes = iota((B, B), 1)
    subs = iota((B, B), 0)
    index_rows[...] = jnp.zeros_like(index_rows)
    index_rows[0:1, 0:TD] = rows_ref[...]
    index_rows[1:2, 0:TD] = cols_ref[...]
    rows = index_rows[0:1, :]
    cols = index_rows[1:2, :]
    row_owner = divided_by_rb(rows)
    col_owner = divided_by_rb(cols)
    row_local = rows - row_owner * RB
    col_local = cols - col_owner * RB
    valid = lane_row < TD
    push = valid & (row_owner != me)
    fetch = valid & (row_owner == me)
    push_f = jnp.where(push, 1.0, 0.0)
    fetch_f = jnp.where(fetch, 1.0, 0.0)
    sub8 = iota((16, B), 0)
    both = jnp.where(sub8 == 0, push_f, jnp.where(sub8 == 1, fetch_f, 0.0))
    ranks = dot(both.astype(BF16), jnp.where(subs < lanes, 1.0, 0.0).astype(BF16))
    position = jnp.where(
        push, ranks[0:1], jnp.where(fetch, ranks[1:2] + HALF, 1000.0)
    ).astype(jnp.int32)
    order = jnp.where(position == subs, 1.0, 0.0).astype(BF16)

    def as_f(v):
        return v.astype(F32)

    destination = jnp.where(push, row_owner, col_owner)
    wanted = jnp.where(fetch, as_f(col_local) + 1.0, 0.0)
    target = jnp.where(push, as_f(row_local) + 1.0, 0.0)
    table = jnp.zeros((B, B), F32)
    for at, value in enumerate(
        (wanted, target, as_f(destination), as_f(col_local), as_f(row_local), as_f(lane_row))
    ):
        table = jnp.where(subs == at, value, table)
    table = table.astype(BF16)
    by_lane = dot_nt(table, order)
    by_sub = dot_nt(order, table)
    dest_lane = by_lane[2:3].astype(jnp.int32)
    row_local_lane = by_lane[4:5].astype(jnp.int32)
    perm_vmem[...] = by_lane[5:6].astype(jnp.int32)
    to_smem = pltpu.make_async_copy(perm_vmem, perm_smem, perm_sem)
    to_smem.start()

    sends_to = jnp.where((dest_lane == subs) & (lanes < TD), 1.0, 0.0)
    push_out = jnp.where(lanes < HALF, sends_to, 0.0).astype(BF16)
    oh_push_out[:, 0:B] = push_out
    oh_push_out[:, B:] = push_out
    dest_sub = by_sub[HALF:TD, 2:3].astype(jnp.int32)
    oh_fetch_in[...] = jnp.where(dest_sub == lanes[0:HALF], 1.0, 0.0).astype(BF16)
    col_local_sub = by_sub[0:HALF, 3:4].astype(jnp.int32)
    oh_cols[...] = jnp.where(col_local_sub == iota((HALF, 16), 1), 1.0, 0.0).astype(BF16)
    lanes16 = iota((16, B), 1)
    local_target = jnp.where(
        (lanes16 >= HALF) & (lanes16 < TD),
        row_local_lane,
        jnp.where((lanes16 >= TD) & (lanes16 < TD + RB), lanes16 - TD, -1),
    )
    local = jnp.where(local_target == sub8, 1.0, 0.0).astype(BF16)
    oh_local[:, 0:B] = local
    oh_local[:, B:] = local

    ysplit[...] = jnp.zeros_like(ysplit)
    products[...] = jnp.zeros_like(products)
    zeros4 = jnp.zeros((4, B), F32)
    u0 = jnp.concatenate([-defect_ref[...], zeros4], axis=0)
    mass = jnp.concatenate([mass_ref[...] - SHIFT, zeros4], axis=0)
    beta_part = total(u0 * u0)
    message = dot(sends_to.astype(BF16), by_sub.astype(BF16))
    req_out[...] = jnp.where(lanes < 2, message, jnp.where(lanes == 2, beta_part, 0.0))

    pl.semaphore_wait(barrier, N - 1)

    def send(source, landing, at):
        for peer in peers:
            pltpu.make_async_remote_copy(
                src_ref=source(peer), dst_ref=landing(me),
                send_sem=send_sem.at[at], recv_sem=recv_sem.at[at],
                device_id=(peer,), device_id_type=MESH,
            ).start()

    def received(ref, at):
        pltpu.make_async_copy(ref, ref, recv_sem.at[at]).wait()

    def sent(ref, at):
        pltpu.make_async_copy(ref, ref, send_sem.at[at]).wait()

    one_row = pl.ds(0, N - 1)
    send(lambda p: req_out.at[pl.ds(p, 1)], lambda m: req_in.at[pl.ds(m, 1)], 0)

    for load in loads:
        load.wait()
    to_smem.wait()

    def put(pair, tile, at):
        high, low = halves(tile.T)
        weights[pair, 0:B, at * B : (at + 1) * B] = high
        weights[pair, B:, at * B : (at + 1) * B] = low

    def in_order(at):
        return raw[jnp.minimum(jnp.maximum(perm_smem[0, at], 0), TD - 1)]

    def prepare(pair, carry):
        put(pair, in_order(2 * pair), 0)
        put(pair, in_order(2 * pair + 1), 1)
        return carry

    lax.fori_loop(0, HALF, prepare, 0)

    def prepare_diag(pair, carry):
        put(HALF + pair, raw_diag[2 * pair], 0)
        put(HALF + pair, raw_diag[2 * pair + 1], 1)
        return carry

    lax.fori_loop(0, RB // 2, prepare_diag, 0)

    rows16 = iota((16, B), 0)

    def tile_products(high, low, first_pair, pairs):
        lhs = jnp.concatenate(
            [jnp.concatenate([high, high], axis=1), jnp.concatenate([low, low], axis=1)], axis=0
        )
        out = jnp.zeros((16, B), F32)
        for i in range(pairs):
            got = dot(lhs, weights[first_pair + i])
            got = got[0:16] + got[16:32]
            out = jnp.where(
                rows16 == 2 * i, got[:, 0:B], jnp.where(rows16 == 2 * i + 1, got[:, B:], out)
            )
        return out

    def push_products(high, low, at):
        picked = dot(oh_cols[...], jnp.concatenate([high, low], axis=1))
        picked = picked.astype(BF16)
        for b in range(3):
            block = picked[16 * b : 16 * b + 16]
            products[16 * b : 16 * b + 16] = tile_products(
                block[:, 0:B], block[:, B:], 8 * b, 8
            )
        p_high, p_low = halves(products[...])
        p_out[at] = dot(oh_push_out[...], jnp.concatenate([p_high, p_low], axis=0))
        send(
            lambda p: p_out.at[at, pl.ds(p, 1)], lambda m: p_in.at[at, pl.ds(m, 1)], 4 + at
        )

    def send_x(vector, high, low, dots_row, at):
        rest = (vector - high.astype(F32) - low.astype(F32)).astype(BF16)
        ysplit[0:16] = high
        ysplit[16:32] = low
        ysplit[32:48] = rest
        x_out[at, 0] = dot(oh_fetch_out[...], ysplit[...])
        x_out[at, 1] = jnp.broadcast_to(dots_row, (B, B))
        send(
            lambda p: x_out.at[at, :, pl.ds(p, 1)],
            lambda m: x_in.at[at, :, pl.ds(m, 1)],
            1 + at,
        )

    def finish(vector, high, low, at):
        products[TD : TD + 16] = tile_products(high, low, HALF, RB // 2)
        received(x_in.at[at, :, one_row], 1 + at)
        x_high, x_low = halves(x_in[at, 0])
        picked = dot(oh_fetch_in[...], jnp.concatenate([x_high, x_low], axis=1))
        picked = picked.astype(BF16)
        for b in range(3):
            block = picked[16 * b : 16 * b + 16]
            products[HALF + 16 * b : HALF + 16 * b + 16] = tile_products(
                block[:, 0:B], block[:, B:], 24 + 8 * b, 8
            )
        p_high, p_low = halves(products[...])
        here = mass * vector + dot(oh_local[...], jnp.concatenate([p_high, p_low], axis=0))
        received(p_in.at[at, one_row], 4 + at)
        p_high, p_low = halves(p_in[at])
        return here + dot(oh_push_in[...], jnp.concatenate([p_high, p_low], axis=0))

    def packed(values):
        row = jnp.zeros((1, B), F32)
        for i, value in enumerate(values):
            row = jnp.where(lane_row == i, value, row)
        return row

    def unpacked(row, count):
        return [
            jnp.sum(jnp.where(lane_row == i, row, 0.0), axis=1, keepdims=True)
            for i in range(count)
        ]

    u_high, u_low = halves(u0)
    push_products(u_high, u_low, 0)
    received(req_in.at[one_row], 0)
    req = req_in[...]
    slot = lanes % 16
    asked = req[:, 0:1].astype(jnp.int32) - 1
    oh_fetch_out[...] = jnp.where((asked == slot) & (lanes < 48), 1.0, 0.0).astype(BF16)
    send_x(u0, u_high, u_low, jnp.zeros((1, B), F32), 0)
    landing = req[:, 1:2].astype(jnp.int32) - 1
    into = jnp.where(landing == lanes, 1.0, 0.0).T[0:16].astype(BF16)
    oh_push_in[:, 0:B] = into
    oh_push_in[:, B:] = into
    beta_row = jnp.where(lane_row == 2, jnp.sum(req, axis=0, keepdims=True), 0.0)
    beta = jnp.sqrt(jnp.sum(beta_row, axis=1, keepdims=True) + beta_part)
    v0 = u0 / beta
    w0 = finish(u0, u_high, u_low, 0) / beta

    def apply_with_dots(vector, others, at):
        row = packed([total(other * vector) for other in others] + [total(vector * vector)])
        high, low = halves(vector)
        send_x(vector, high, low, row, at)
        push_products(high, low, at)
        image = finish(vector, high, low, at)
        sums = jnp.sum(x_in[at, 1], axis=0, keepdims=True) + row
        return image, unpacked(sums, len(others) + 1)

    z1, (h00, square) = apply_with_dots(w0, [v0], 1)
    h10 = jnp.sqrt(square - h00 * h00)
    v1 = (w0 - h00 * v0) / h10
    w1 = (z1 - h00 * w0) / h10

    z2, (h01, h11, square) = apply_with_dots(w1, [v0, v1], 2)
    h21 = jnp.sqrt(square - h01 * h01 - h11 * h11)
    v2 = (w1 - h01 * v0 - h11 * v1) / h21
    w2 = (z2 - h01 * w0 - h11 * w1) / h21

    row = packed([total(v0 * w2), total(v1 * w2), total(v2 * w2), total(w2 * w2)])
    f_out[...] = jnp.broadcast_to(row, (8, B))
    send(lambda p: f_out.at[pl.ds(0, 1)], lambda m: f_in.at[pl.ds(m, 1)], 7)
    received(f_in.at[one_row], 7)
    sums = jnp.sum(f_in[...], axis=0, keepdims=True) + row
    h02, h12, h22, square = unpacked(sums, 4)
    h32 = jnp.sqrt(square - h02 * h02 - h12 * h12 - h22 * h22)

    h00, h11, h22 = h00 + SHIFT, h11 + SHIFT, h22 + SHIFT
    g00 = h00 * h00 + h10 * h10
    g10 = h01 * h00 + h11 * h10
    g20 = h02 * h00 + h12 * h10
    g11 = h01 * h01 + h11 * h11 + h21 * h21
    g21 = h02 * h01 + h12 * h11 + h22 * h21
    g22 = h02 * h02 + h12 * h12 + h22 * h22 + h32 * h32
    l00 = jnp.sqrt(g00)
    l10, l20 = g10 / l00, g20 / l00
    l11 = jnp.sqrt(g11 - l10 * l10)
    l21 = (g21 - l20 * l10) / l11
    l22 = jnp.sqrt(g22 - l20 * l20 - l21 * l21)
    t0 = beta * h00 / l00
    t1 = (beta * h01 - l10 * t0) / l11
    t2 = (beta * h02 - l20 * t0 - l21 * t1) / l22
    m2 = t2 / l22
    m1 = (t1 - l21 * m2) / l11
    m0 = (t0 - l10 * m1 - l20 * m2) / l00
    update = m0 * v0 + m1 * v1 + m2 * v2
    out_ref[...] = update[0:RB]

    sent(req_out.at[one_row], 0)
    for at in range(3):
        sent(x_out.at[at, :, one_row], 1 + at)
        sent(p_out.at[at, one_row], 4 + at)
    sent(f_in.at[one_row], 7)


def on_device(defect, mass, block_diag, coupling, tile_rows, tile_cols):
    vmem = pl.BlockSpec(memory_space=pltpu.VMEM)
    hbm = pl.BlockSpec(memory_space=pl.ANY)
    return pl.pallas_call(
        kernel,
        out_shape=jax.ShapeDtypeStruct(defect.shape, F32),
        in_specs=[vmem, vmem, hbm, hbm, vmem, vmem],
        out_specs=vmem,
        scratch_shapes=[
            pltpu.VMEM((TD, B, B), F32),
            pltpu.VMEM((RB, B, B), F32),
            pltpu.VMEM((54, 2 * B, 2 * B), BF16),
            pltpu.VMEM((8, B), jnp.int32),
            pltpu.VMEM((1, B), jnp.int32),
            pltpu.SMEM((1, B), jnp.int32),
            pltpu.VMEM((B, B), BF16),
            pltpu.VMEM((B, B), F32),
            pltpu.VMEM((B, B), BF16),
            pltpu.VMEM((16, 2 * B), BF16),
            pltpu.VMEM((HALF, 16), BF16),
            pltpu.VMEM((B, 2 * B), BF16),
            pltpu.VMEM((16, 2 * B), BF16),
            pltpu.VMEM((HALF, B), BF16),
            pltpu.VMEM((N, B), F32),
            pltpu.VMEM((N, B), F32),
            pltpu.VMEM((3, 2, N, B), F32),
            pltpu.VMEM((3, 2, N, B), F32),
            pltpu.VMEM((3, N, B), F32),
            pltpu.VMEM((3, N, B), F32),
            pltpu.VMEM((8, B), F32),
            pltpu.VMEM((N, B), F32),
            pltpu.SemaphoreType.DMA((7,)),
            pltpu.SemaphoreType.DMA,
            pltpu.SemaphoreType.DMA((8,)),
            pltpu.SemaphoreType.DMA((8,)),
        ],
        compiler_params=pltpu.CompilerParams(collective_id=0, has_side_effects=True),
    )(
        defect, mass, block_diag, coupling,
        tile_rows.reshape(1, TD), tile_cols.reshape(1, TD),
    )


def solution(mesh):
    return jax.shard_map(
        on_device,
        mesh=mesh,
        in_specs=(
            P("blk", None),
            P("blk", None),
            P("blk", None, None),
            P("blk", None, None),
            P("blk"),
            P("blk"),
        ),
        out_specs=P("blk", None),
        check_vma=False,
    )
```

time: 320 us -> 50.5 us (0.16)
  blocking collectives: 129 us -> 0 us
  Pallas kernels: 0 us -> 49 us
  waiting for transfers between devices: 48 us -> 0 us
  matrix products: 42.5 us -> 0 us
  starting transfers between devices: 41.6 us -> 0 us
  other arithmetic: 20.6 us -> 0 us
  local copies, waits for them, and re-layouts: 21.8 us -> 1.3 us
  between operations: 15.3 us -> 0.01 us
    psum x16 -> x0, blocking collectives: 129 us -> none  [one_axis_at_a_time(): return functools.reduce(lax.psum, axes, x)]
    pallas_call x0 -> x1, Pallas kernels: none -> 49 us  [on_device(): pl.pallas_call(kernel, out_shape=jax.ShapeDtypeStruct(defect.shape, F32),...]
    all_to_all x7 -> x0, waiting for transfers between devices: 48 us -> none  [the longest x3 28.2 us: on_device(): lax.all_to_all(outgoing, BLK, split_axis=0, concat_axis=0, tiled=True)]
    dot_general x13 -> x0, matrix products: 42.5 us -> none  [the longest x3 35.5 us: tile_products(): jnp.einsum('tij,tj->ti', coupling, inputs, precision=lax.Precision.HIGHEST)]
    all_to_all x7 -> x0, starting transfers between devices: 41.6 us -> none  [the longest x3 16.5 us: on_device(): lax.all_to_all(apply_vector[asked], BLK, split_axis=0, concat_axis=0, til...]
    another operation x12 -> x0, other arithmetic: 10.4 us -> none
    scatter x11 -> x0, local copies, waits for them, and re-layouts: 9.84 us -> none  [the longest x3 4.17 us: on_device(): outgoing = jnp.zeros((devices, slots, width), jnp.float32).at[push_lane,...]
    gather x9 -> x0, local copies, waits for them, and re-layouts: 8.01 us -> none  [the longest x3 3.69 us: on_device(): apply_vector[asked]]
  transfers between devices with their start and end apart: 7 -> 0, of which waited for: 6 -> 0; matrix products, arithmetic and copies ran while one was open for 5% -> 0% of each run, Pallas kernels for 0% -> 0%
where the time goes in v1:
time: 50.5 us; the launch traced here: 50.3 us
  Pallas kernels  49 us (97%)
  local copies, waits for them, and re-layouts  1.3 us (3%)
    pallas_call x1, Pallas kernels, on_device(): pl.pallas_call(kernel, out_shape=jax.ShapeDtypeStruct(defect.shape, F32),...  49 us
    unnamed x1, local copies, waits for them, and re-layouts  1.3 us

profile of v1, /device:TPU:1, one launch (start us, length us, event | category | flops | bytes accessed | tf_op | source)
XLA Modules:
  0.0 50.3 jit_solution(6365415423096293249)
XLA Ops:
  0.0 49.0 %shard_map.64 = f32[12,128]{1,0:T(8,128)} custom-call(f32[12,128]{1,0:T(8,128)} %defect_ref.1, f32[12,128]{1,0:T(8,128)} %mass_ref.1, f32[12,128,128]{2,1,0:T(8,128)} %diag_hbm.1, f32[96,128,128]{2,1,0:T(8,128)} %coup_hbm.1, s32[1,96]{1,0:T(1,128)} %bitcast.2, s32[1,96]{1,0:T(1,128)} %bitcast.3), custom_call_target="tpu_custom_call" | custom-call | tf_op jit(solution)/shard_map/pallas_call | solution.py:357
  49.0 1.3 %copy.8 = f32[12,128]{1,0:T(8,128)} copy(f32[12,128]{1,0:T(8,128)} %shard_map.64) | data formatting | bytes 12288

commit v2 on v1

--- a/solution.py
+++ b/solution.py
@@ -56,11 +56,11 @@
 
 
 def kernel(
-    defect_ref, mass_ref, diag_hbm, coup_hbm, rows_ref, cols_ref, out_ref,
-    raw, raw_diag, weights, index_rows, perm_vmem, perm_smem,
+    defect_hbm, mass_hbm, diag_hbm, coup_hbm, rows_hbm, cols_hbm, out_ref,
+    indices, vectors, raw, raw_diag, weights, index_rows, perm_vmem, perm_smem,
     ysplit, products, oh_fetch_out, oh_push_in, oh_cols, oh_push_out, oh_local, oh_fetch_in,
     req_out, req_in, x_out, x_in, p_out, p_in, f_out, f_in,
-    load_sem, perm_sem, send_sem, recv_sem,
+    load_sem, small_sem, perm_sem, send_sem, recv_sem,
 ):
     me = lax.axis_index("blk")
     y, z, x, c = me // 32, (me // 8) % 4, (me // 2) % 4, me % 2
@@ -72,15 +72,27 @@
     xc = [[x_part[a] + c_part[b] for b in range(2)] for a in range(4)]
     peers = [yz[o[0]][o[1]] + xc[o[2]][o[3]] for o in OFFSETS]
 
-    req_in[...] = jnp.zeros_like(req_in)
-    x_in[...] = jnp.zeros_like(x_in)
-    p_in[...] = jnp.zeros_like(p_in)
-    f_in[...] = jnp.zeros_like(f_in)
+    mine = pl.ds(me, 1)
+    nothing = jnp.zeros((1, B), F32)
+    req_in[mine] = nothing
+    f_in[mine] = nothing
+    for at in range(3):
+        x_in[at, 0, mine] = nothing
+        x_in[at, 1, mine] = nothing
+        p_in[at, mine] = nothing
 
     barrier = pltpu.get_barrier_semaphore()
     for peer in peers:
         pl.semaphore_signal(barrier, inc=1, device_id=(peer,), device_id_type=MESH)
 
+    small_loads = [
+        pltpu.make_async_copy(rows_hbm, indices.at[0], small_sem.at[0]),
+        pltpu.make_async_copy(cols_hbm, indices.at[1], small_sem.at[1]),
+        pltpu.make_async_copy(defect_hbm, vectors.at[0, 0:RB], small_sem.at[2]),
+        pltpu.make_async_copy(mass_hbm, vectors.at[1, 0:RB], small_sem.at[3]),
+    ]
+    for load in small_loads:
+        load.start()
     loads = [
         pltpu.make_async_copy(
             coup_hbm.at[pl.ds(16 * i, 16)], raw.at[pl.ds(16 * i, 16)], load_sem.at[i]
@@ -94,9 +106,13 @@
     lane_row = iota((1, B), 1)
     lanes = iota((B, B), 1)
     subs = iota((B, B), 0)
+    ysplit[...] = jnp.zeros_like(ysplit)
+    products[...] = jnp.zeros_like(products)
+    for load in small_loads:
+        load.wait()
     index_rows[...] = jnp.zeros_like(index_rows)
-    index_rows[0:1, 0:TD] = rows_ref[...]
-    index_rows[1:2, 0:TD] = cols_ref[...]
+    index_rows[0:1, 0:TD] = indices[0]
+    index_rows[1:2, 0:TD] = indices[1]
     rows = index_rows[0:1, :]
     cols = index_rows[1:2, :]
     row_owner = divided_by_rb(rows)
@@ -154,11 +170,9 @@
     oh_local[:, 0:B] = local
     oh_local[:, B:] = local
 
-    ysplit[...] = jnp.zeros_like(ysplit)
-    products[...] = jnp.zeros_like(products)
-    zeros4 = jnp.zeros((4, B), F32)
-    u0 = jnp.concatenate([-defect_ref[...], zeros4], axis=0)
-    mass = jnp.concatenate([mass_ref[...] - SHIFT, zeros4], axis=0)
+    own_rows = iota((16, B), 0) < RB
+    u0 = jnp.where(own_rows, -vectors[0], 0.0)
+    mass = jnp.where(own_rows, vectors[1] - SHIFT, 0.0)
     beta_part = total(u0 * u0)
     message = dot(sends_to.astype(BF16), by_sub.astype(BF16))
     req_out[...] = jnp.where(lanes < 2, message, jnp.where(lanes == 2, beta_part, 0.0))
@@ -194,19 +208,12 @@
     def in_order(at):
         return raw[jnp.minimum(jnp.maximum(perm_smem[0, at], 0), TD - 1)]
 
-    def prepare(pair, carry):
+    for pair in range(HALF):
         put(pair, in_order(2 * pair), 0)
         put(pair, in_order(2 * pair + 1), 1)
-        return carry
-
-    lax.fori_loop(0, HALF, prepare, 0)
-
-    def prepare_diag(pair, carry):
+    for pair in range(RB // 2):
         put(HALF + pair, raw_diag[2 * pair], 0)
         put(HALF + pair, raw_diag[2 * pair + 1], 1)
-        return carry
-
-    lax.fori_loop(0, RB // 2, prepare_diag, 0)
 
     rows16 = iota((16, B), 0)
 
@@ -356,10 +363,12 @@
     hbm = pl.BlockSpec(memory_space=pl.ANY)
     return pl.pallas_call(
         kernel,
-        out_shape=jax.ShapeDtypeStruct(defect.shape, F32),
-        in_specs=[vmem, vmem, hbm, hbm, vmem, vmem],
+        out_shape=pltpu.VMEM(defect.shape, F32),
+        in_specs=[hbm] * 6,
         out_specs=vmem,
         scratch_shapes=[
+            pltpu.VMEM((2, 1, TD), jnp.int32),
+            pltpu.VMEM((2, 16, B), F32),
             pltpu.VMEM((TD, B, B), F32),
             pltpu.VMEM((RB, B, B), F32),
             pltpu.VMEM((54, 2 * B, 2 * B), BF16),
@@ -383,6 +392,7 @@
             pltpu.VMEM((8, B), F32),
             pltpu.VMEM((N, B), F32),
             pltpu.SemaphoreType.DMA((7,)),
+            pltpu.SemaphoreType.DMA((4,)),
             pltpu.SemaphoreType.DMA,
             pltpu.SemaphoreType.DMA((8,)),
             pltpu.SemaphoreType.DMA((8,)),

time: 50.5 us -> 45.5 us (0.901)
  Pallas kernels: 49 us -> 44.8 us
  local copies, waits for them, and re-layouts: 1.3 us -> 0.6 us
    pallas_call x1, Pallas kernels: 49 us -> 44.8 us  [on_device(): pl.pallas_call(kernel, out_shape=pltpu.VMEM(defect.shape, F32), in_specs=...]
    unnamed x1, local copies, waits for them, and re-layouts: 1.3 us -> 0.6 us
where the time goes in v2:
time: 45.5 us; the launch traced here: 45.4 us
  Pallas kernels  44.8 us (98%)
  local copies, waits for them, and re-layouts  0.6 us (1%)
    pallas_call x1, Pallas kernels, on_device(): pl.pallas_call(kernel, out_shape=pltpu.VMEM(defect.shape, F32), in_specs=...  44.8 us

profile of v2, /device:TPU:1, one launch (start us, length us, event | category | flops | bytes accessed | tf_op | source)
XLA Modules:
  0.0 45.4 jit_solution(17802790283558363)
XLA Ops:
  0.0 44.8 %shard_map.64 = f32[12,128]{1,0:T(8,128)S(1)} custom-call(f32[12,128]{1,0:T(8,128)} %defect_hbm.1, f32[12,128]{1,0:T(8,128)} %mass_hbm.1, f32[12,128,128]{2,1,0:T(8,128)} %diag_hbm.1, f32[96,128,128]{2,1,0:T(8,128)} %coup_hbm.1, s32[1,96]{1,0:T(1,128)} %bitcast.2, s32[1,96]{1,0:T(1,128)} %bitcast.3), custom_call_target="tpu_custom_call" | custom-call | tf_op jit(solution)/shard_map/pallas_call | solution.py:364
  44.8 0.6 %copy.8 = f32[12,128]{1,0:T(8,128)} copy(f32[12,128]{1,0:T(8,128)S(1)} %shard_map.64) | data formatting | bytes 12288

commit v3 on v2

--- a/solution.py
+++ b/solution.py
@@ -29,6 +29,18 @@
 )
 
 
+def code(offset):
+    return offset[0] * 32 + offset[1] * 8 + offset[2] * 2 + offset[3]
+
+
+def opposite(offset):
+    return tuple((4 - step) % 4 for step in offset[:3]) + (offset[3],)
+
+
+FAR = 14
+FAR_CODES = [code(o) for o in OFFSETS[:FAR]]
+
+
 def dot(a, b):
     return lax.dot_general(a, b, (((1,), (0,)), ((), ())), preferred_element_type=F32)
 
@@ -58,8 +70,8 @@
 def kernel(
     defect_hbm, mass_hbm, diag_hbm, coup_hbm, rows_hbm, cols_hbm, out_ref,
     indices, vectors, raw, raw_diag, weights, index_rows, perm_vmem, perm_smem,
-    ysplit, products, oh_fetch_out, oh_push_in, oh_cols, oh_push_out, oh_local, oh_fetch_in,
-    req_out, req_in, x_out, x_in, p_out, p_in, f_out, f_in,
+    products, oh_fetch_out, oh_push_in, oh_cols, oh_push_out, oh_local,
+    oh_fetch_in, req_out, req_in, xp_out, xp_in, x_far, f_out, f_in,
     load_sem, small_sem, perm_sem, send_sem, recv_sem,
 ):
     me = lax.axis_index("blk")
@@ -72,27 +84,12 @@
     xc = [[x_part[a] + c_part[b] for b in range(2)] for a in range(4)]
     peers = [yz[o[0]][o[1]] + xc[o[2]][o[3]] for o in OFFSETS]
 
-    mine = pl.ds(me, 1)
-    nothing = jnp.zeros((1, B), F32)
-    req_in[mine] = nothing
-    f_in[mine] = nothing
-    for at in range(3):
-        x_in[at, 0, mine] = nothing
-        x_in[at, 1, mine] = nothing
-        p_in[at, mine] = nothing
-
-    barrier = pltpu.get_barrier_semaphore()
-    for peer in peers:
-        pl.semaphore_signal(barrier, inc=1, device_id=(peer,), device_id_type=MESH)
-
     small_loads = [
         pltpu.make_async_copy(rows_hbm, indices.at[0], small_sem.at[0]),
         pltpu.make_async_copy(cols_hbm, indices.at[1], small_sem.at[1]),
         pltpu.make_async_copy(defect_hbm, vectors.at[0, 0:RB], small_sem.at[2]),
         pltpu.make_async_copy(mass_hbm, vectors.at[1, 0:RB], small_sem.at[3]),
     ]
-    for load in small_loads:
-        load.start()
     loads = [
         pltpu.make_async_copy(
             coup_hbm.at[pl.ds(16 * i, 16)], raw.at[pl.ds(16 * i, 16)], load_sem.at[i]
@@ -100,13 +97,22 @@
         for i in range(6)
     ]
     loads.append(pltpu.make_async_copy(diag_hbm, raw_diag, load_sem.at[6]))
-    for load in loads:
+    for load in small_loads + loads:
         load.start()
+
+    nothing = jnp.zeros((1, B), F32)
+    req_in[0:1] = nothing
+    f_in[0:1] = nothing
+    xp_in[...] = jnp.zeros_like(xp_in)
+    x_far[...] = jnp.zeros_like(x_far)
+
+    barrier = pltpu.get_barrier_semaphore()
+    for peer in peers:
+        pl.semaphore_signal(barrier, inc=1, device_id=(peer,), device_id_type=MESH)
 
     lane_row = iota((1, B), 1)
     lanes = iota((B, B), 1)
     subs = iota((B, B), 0)
-    ysplit[...] = jnp.zeros_like(ysplit)
     products[...] = jnp.zeros_like(products)
     for load in small_loads:
         load.wait()
@@ -117,25 +123,40 @@
     cols = index_rows[1:2, :]
     row_owner = divided_by_rb(rows)
     col_owner = divided_by_rb(cols)
+
+    def hop(d):
+        return jnp.where(d == 3, 1, d)
+
+    def relative(owner):
+        dy = (lax.shift_right_logical(owner, 5) - y) & 3
+        dz = (lax.shift_right_logical(owner, 3) - z) & 3
+        dx = (lax.shift_right_logical(owner, 1) - x) & 3
+        dc = (owner + c) & 1
+        return dy * 32 + dz * 8 + dx * 2 + dc, hop(dy) + hop(dz) + hop(dx) >= 5
+
     row_local = rows - row_owner * RB
     col_local = cols - col_owner * RB
     valid = lane_row < TD
     push = valid & (row_owner != me)
     fetch = valid & (row_owner == me)
-    push_f = jnp.where(push, 1.0, 0.0)
-    fetch_f = jnp.where(fetch, 1.0, 0.0)
+    destination, is_far = relative(jnp.where(push, row_owner, col_owner))
     sub8 = iota((16, B), 0)
-    both = jnp.where(sub8 == 0, push_f, jnp.where(sub8 == 1, fetch_f, 0.0))
-    ranks = dot(both.astype(BF16), jnp.where(subs < lanes, 1.0, 0.0).astype(BF16))
-    position = jnp.where(
-        push, ranks[0:1], jnp.where(fetch, ranks[1:2] + HALF, 1000.0)
-    ).astype(jnp.int32)
+    kinds = [push & is_far, push & ~is_far, fetch & ~is_far, fetch & is_far]
+    members = jnp.zeros((16, B), F32)
+    for at, kind in enumerate(kinds):
+        members = jnp.where((sub8 == at) & kind, 1.0, members)
+    counts = jnp.sum(members, axis=1, keepdims=True)
+    ranks = dot(members.astype(BF16), jnp.where(subs < lanes, 1.0, 0.0).astype(BF16))
+    starts = [0.0, counts[0:1], HALF * 1.0, counts[2:3] + HALF]
+    position = jnp.full((1, B), 1000.0, F32)
+    for at, kind in enumerate(kinds):
+        position = jnp.where(kind, ranks[at : at + 1] + starts[at], position)
+    position = position.astype(jnp.int32)
     order = jnp.where(position == subs, 1.0, 0.0).astype(BF16)
 
     def as_f(v):
         return v.astype(F32)
 
-    destination = jnp.where(push, row_owner, col_owner)
     wanted = jnp.where(fetch, as_f(col_local) + 1.0, 0.0)
     target = jnp.where(push, as_f(row_local) + 1.0, 0.0)
     table = jnp.zeros((B, B), F32)
@@ -156,8 +177,13 @@
     push_out = jnp.where(lanes < HALF, sends_to, 0.0).astype(BF16)
     oh_push_out[:, 0:B] = push_out
     oh_push_out[:, B:] = push_out
+    slot = lanes % 16
     dest_sub = by_sub[HALF:TD, 2:3].astype(jnp.int32)
-    oh_fetch_in[...] = jnp.where(dest_sub == lanes[0:HALF], 1.0, 0.0).astype(BF16)
+    oh_fetch_in[:, 0:B] = jnp.where(dest_sub == lanes[0:HALF], 1.0, 0.0).astype(BF16)
+    far_codes = jnp.full((1, B), -1, jnp.int32)
+    for at, value in enumerate(FAR_CODES):
+        far_codes = jnp.where(lane_row == at, value, far_codes)
+    oh_fetch_in[:, B:] = jnp.where(dest_sub == far_codes, 1.0, 0.0).astype(BF16)
     col_local_sub = by_sub[0:HALF, 3:4].astype(jnp.int32)
     oh_cols[...] = jnp.where(col_local_sub == iota((HALF, 16), 1), 1.0, 0.0).astype(BF16)
     lanes16 = iota((16, B), 1)
@@ -179,13 +205,17 @@
 
     pl.semaphore_wait(barrier, N - 1)
 
-    def send(source, landing, at):
-        for peer in peers:
-            pltpu.make_async_remote_copy(
-                src_ref=source(peer), dst_ref=landing(me),
-                send_sem=send_sem.at[at], recv_sem=recv_sem.at[at],
-                device_id=(peer,), device_id_type=MESH,
-            ).start()
+    def send_one(source, landing, at, k):
+        offset = OFFSETS[k]
+        pltpu.make_async_remote_copy(
+            src_ref=source(code(offset)), dst_ref=landing(code(opposite(offset))),
+            send_sem=send_sem.at[at], recv_sem=recv_sem.at[at],
+            device_id=(peers[k],), device_id_type=MESH,
+        ).start()
+
+    def send(source, landing, at, first=0, last=N - 1):
+        for k in range(first, last):
+            send_one(source, landing, at, k)
 
     def received(ref, at):
         pltpu.make_async_copy(ref, ref, recv_sem.at[at]).wait()
@@ -194,7 +224,9 @@
         pltpu.make_async_copy(ref, ref, send_sem.at[at]).wait()
 
     one_row = pl.ds(0, N - 1)
-    send(lambda p: req_out.at[pl.ds(p, 1)], lambda m: req_in.at[pl.ds(m, 1)], 0)
+    far_rows = pl.ds(0, FAR)
+    rest_rows = pl.ds(0, N - 1 - FAR)
+    send(lambda p: req_out.at[p : p + 1], lambda m: req_in.at[m : m + 1], 0)
 
     for load in loads:
         load.wait()
@@ -217,62 +249,90 @@
 
     rows16 = iota((16, B), 0)
 
-    def tile_products(high, low, first_pair, pairs):
+    def tile_products(high, low, first_pair, pairs, between=lambda: None):
         lhs = jnp.concatenate(
             [jnp.concatenate([high, high], axis=1), jnp.concatenate([low, low], axis=1)], axis=0
         )
         out = jnp.zeros((16, B), F32)
         for i in range(pairs):
             got = dot(lhs, weights[first_pair + i])
+            between()
             got = got[0:16] + got[16:32]
             out = jnp.where(
                 rows16 == 2 * i, got[:, 0:B], jnp.where(rows16 == 2 * i + 1, got[:, B:], out)
             )
         return out
 
-    def push_products(high, low, at):
-        picked = dot(oh_cols[...], jnp.concatenate([high, low], axis=1))
-        picked = picked.astype(BF16)
+    def block_products(picked, first_pair, between=lambda: None):
+        return tile_products(picked[:, 0:B], picked[:, B:], first_pair, 8, between)
+
+    def send_push(at):
+        send(
+            lambda p: xp_out.at[at, 2, p : p + 1], lambda m: xp_in.at[at, 2, m : m + 1], 4 + at
+        )
+
+    def send_x(at):
+        planes = slice(0, 2) if at else slice(0, 1)
+        send(
+            lambda p: xp_out.at[at, planes, p : p + 1],
+            lambda m: x_far.at[at, planes, FAR_CODES.index(m) : FAR_CODES.index(m) + 1],
+            8 + at, 0, FAR,
+        )
+        left = iter(range(FAR, N - 1))
+
+        def more(count):
+            for k in itertools.islice(left, count):
+                send_one(
+                    lambda p: xp_out.at[at, planes, p : p + 1],
+                    lambda m: xp_in.at[at, planes, m : m + 1], 1 + at, k,
+                )
+
+        return more
+
+    def push(high, low, at, between=lambda: None):
+        picked = dot(oh_cols[...], jnp.concatenate([high, low], axis=1)).astype(BF16)
         for b in range(3):
-            block = picked[16 * b : 16 * b + 16]
-            products[16 * b : 16 * b + 16] = tile_products(
-                block[:, 0:B], block[:, B:], 8 * b, 8
+            products[16 * b : 16 * b + 16] = block_products(
+                picked[16 * b : 16 * b + 16], 8 * b, between
             )
         p_high, p_low = halves(products[...])
-        p_out[at] = dot(oh_push_out[...], jnp.concatenate([p_high, p_low], axis=0))
-        send(
-            lambda p: p_out.at[at, pl.ds(p, 1)], lambda m: p_in.at[at, pl.ds(m, 1)], 4 + at
-        )
-
-    def send_x(vector, high, low, dots_row, at):
+        xp_out[at, 2] = dot(oh_push_out[...], jnp.concatenate([p_high, p_low], axis=0))
+
+    def make_x(vector, high, low, dots_row, at):
         rest = (vector - high.astype(F32) - low.astype(F32)).astype(BF16)
-        ysplit[0:16] = high
-        ysplit[16:32] = low
-        ysplit[32:48] = rest
-        x_out[at, 0] = dot(oh_fetch_out[...], ysplit[...])
-        x_out[at, 1] = jnp.broadcast_to(dots_row, (B, B))
-        send(
-            lambda p: x_out.at[at, :, pl.ds(p, 1)],
-            lambda m: x_in.at[at, :, pl.ds(m, 1)],
-            1 + at,
-        )
-
-    def finish(vector, high, low, at):
+        stacked = jnp.concatenate([high, low, rest], axis=0)
+        xp_out[at, 0] = dot(oh_fetch_out[:, 0:HALF], stacked)
+        if at:
+            xp_out[at, 1] = jnp.broadcast_to(dots_row, (B, B))
+
+    def finish(vector, high, low, at, reduced, images):
+        planes = slice(0, 2) if at else slice(0, 1)
         products[TD : TD + 16] = tile_products(high, low, HALF, RB // 2)
-        received(x_in.at[at, :, one_row], 1 + at)
-        x_high, x_low = halves(x_in[at, 0])
-        picked = dot(oh_fetch_in[...], jnp.concatenate([x_high, x_low], axis=1))
-        picked = picked.astype(BF16)
-        for b in range(3):
-            block = picked[16 * b : 16 * b + 16]
-            products[HALF + 16 * b : HALF + 16 * b + 16] = tile_products(
-                block[:, 0:B], block[:, B:], 24 + 8 * b, 8
+        received(xp_in.at[at, planes, rest_rows], 1 + at)
+        near = jnp.concatenate(halves(xp_in[at, 0]), axis=1)
+        picked = dot(oh_fetch_in[0:32, 0:B], near).astype(BF16)
+        for b in range(2):
+            products[HALF + 16 * b : HALF + 16 * b + 16] = block_products(
+                picked[16 * b : 16 * b + 16], 24 + 8 * b
             )
+        received(x_far.at[at, planes, far_rows], 8 + at)
+        far = jnp.concatenate(halves(x_far[at, 0]), axis=1)
+        picked = dot(oh_fetch_in[32:48, 0:B], near) + dot(oh_fetch_in[32:48, B : B + 16], far)
+        products[HALF + 32 : TD] = block_products(picked.astype(BF16), 40)
         p_high, p_low = halves(products[...])
         here = mass * vector + dot(oh_local[...], jnp.concatenate([p_high, p_low], axis=0))
-        received(p_in.at[at, one_row], 4 + at)
-        p_high, p_low = halves(p_in[at])
-        return here + dot(oh_push_in[...], jnp.concatenate([p_high, p_low], axis=0))
+        sums = reduced()
+        norm = sums[-1]
+        for term, image in zip(sums, images):
+            norm = norm - term * term
+            here = here - term * image
+        norm = jnp.sqrt(norm)
+        scale = 1.0 / norm
+        here = here * scale
+        received(xp_in.at[at, 2, one_row], 4 + at)
+        p_high, p_low = halves(xp_in[at, 2])
+        image = here + scale * dot(oh_push_in[...], jnp.concatenate([p_high, p_low], axis=0))
+        return sums[:-1], norm, scale, image
 
     def packed(values):
         row = jnp.zeros((1, B), F32)
@@ -287,44 +347,47 @@
         ]
 
     u_high, u_low = halves(u0)
-    push_products(u_high, u_low, 0)
+    push(u_high, u_low, 0)
+    send_push(0)
     received(req_in.at[one_row], 0)
     req = req_in[...]
-    slot = lanes % 16
     asked = req[:, 0:1].astype(jnp.int32) - 1
     oh_fetch_out[...] = jnp.where((asked == slot) & (lanes < 48), 1.0, 0.0).astype(BF16)
-    send_x(u0, u_high, u_low, jnp.zeros((1, B), F32), 0)
+    make_x(u0, u_high, u_low, None, 0)
+    send_x(0)(N)
     landing = req[:, 1:2].astype(jnp.int32) - 1
     into = jnp.where(landing == lanes, 1.0, 0.0).T[0:16].astype(BF16)
     oh_push_in[:, 0:B] = into
     oh_push_in[:, B:] = into
     beta_row = jnp.where(lane_row == 2, jnp.sum(req, axis=0, keepdims=True), 0.0)
-    beta = jnp.sqrt(jnp.sum(beta_row, axis=1, keepdims=True) + beta_part)
-    v0 = u0 / beta
-    w0 = finish(u0, u_high, u_low, 0) / beta
-
-    def apply_with_dots(vector, others, at):
+    beta_square = jnp.sum(beta_row, axis=1, keepdims=True) + beta_part
+    _, beta, scale, w0 = finish(u0, u_high, u_low, 0, lambda: [beta_square], [])
+    v0 = u0 * scale
+
+    def apply_with_dots(vector, others, images, at):
         row = packed([total(other * vector) for other in others] + [total(vector * vector)])
         high, low = halves(vector)
-        send_x(vector, high, low, row, at)
-        push_products(high, low, at)
-        image = finish(vector, high, low, at)
-        sums = jnp.sum(x_in[at, 1], axis=0, keepdims=True) + row
-        return image, unpacked(sums, len(others) + 1)
-
-    z1, (h00, square) = apply_with_dots(w0, [v0], 1)
-    h10 = jnp.sqrt(square - h00 * h00)
-    v1 = (w0 - h00 * v0) / h10
-    w1 = (z1 - h00 * w0) / h10
-
-    z2, (h01, h11, square) = apply_with_dots(w1, [v0, v1], 2)
-    h21 = jnp.sqrt(square - h01 * h01 - h11 * h11)
-    v2 = (w1 - h01 * v0 - h11 * v1) / h21
-    w2 = (z2 - h01 * w0 - h11 * w1) / h21
+        make_x(vector, high, low, row, at)
+        more = send_x(at)
+        push(high, low, at, lambda: more(5))
+        more(N)
+        send_push(at)
+
+        def reduced():
+            sums = jnp.sum(xp_in[at, 1], axis=0, keepdims=True) + row
+            sums = sums + jnp.sum(x_far[at, 1], axis=0, keepdims=True)
+            return unpacked(sums, len(others) + 1)
+
+        return finish(vector, high, low, at, reduced, images)
+
+    (h00,), h10, scale, w1 = apply_with_dots(w0, [v0], [w0], 1)
+    v1 = (w0 - h00 * v0) * scale
+    (h01, h11), h21, scale, w2 = apply_with_dots(w1, [v0, v1], [w0, w1], 2)
+    v2 = (w1 - h01 * v0 - h11 * v1) * scale
 
     row = packed([total(v0 * w2), total(v1 * w2), total(v2 * w2), total(w2 * w2)])
     f_out[...] = jnp.broadcast_to(row, (8, B))
-    send(lambda p: f_out.at[pl.ds(0, 1)], lambda m: f_in.at[pl.ds(m, 1)], 7)
+    send(lambda p: f_out.at[0:1], lambda m: f_in.at[m : m + 1], 7)
     received(f_in.at[one_row], 7)
     sums = jnp.sum(f_in[...], axis=0, keepdims=True) + row
     h02, h12, h22, square = unpacked(sums, 4)
@@ -353,8 +416,10 @@
 
     sent(req_out.at[one_row], 0)
     for at in range(3):
-        sent(x_out.at[at, :, one_row], 1 + at)
-        sent(p_out.at[at, one_row], 4 + at)
+        planes = slice(0, 2) if at else slice(0, 1)
+        sent(xp_in.at[at, planes, rest_rows], 1 + at)
+        sent(x_far.at[at, planes, far_rows], 8 + at)
+        sent(xp_in.at[at, 2, one_row], 4 + at)
     sent(f_in.at[one_row], 7)
 
 
@@ -375,27 +440,25 @@
             pltpu.VMEM((8, B), jnp.int32),
             pltpu.VMEM((1, B), jnp.int32),
             pltpu.SMEM((1, B), jnp.int32),
-            pltpu.VMEM((B, B), BF16),
             pltpu.VMEM((B, B), F32),
             pltpu.VMEM((B, B), BF16),
             pltpu.VMEM((16, 2 * B), BF16),
             pltpu.VMEM((HALF, 16), BF16),
             pltpu.VMEM((B, 2 * B), BF16),
             pltpu.VMEM((16, 2 * B), BF16),
-            pltpu.VMEM((HALF, B), BF16),
+            pltpu.VMEM((HALF, 2 * B), BF16),
             pltpu.VMEM((N, B), F32),
             pltpu.VMEM((N, B), F32),
-            pltpu.VMEM((3, 2, N, B), F32),
-            pltpu.VMEM((3, 2, N, B), F32),
-            pltpu.VMEM((3, N, B), F32),
-            pltpu.VMEM((3, N, B), F32),
+            pltpu.VMEM((3, 3, N, B), F32),
+            pltpu.VMEM((3, 3, N, B), F32),
+            pltpu.VMEM((3, 2, 16, B), F32),
             pltpu.VMEM((8, B), F32),
             pltpu.VMEM((N, B), F32),
             pltpu.SemaphoreType.DMA((7,)),
             pltpu.SemaphoreType.DMA((4,)),
             pltpu.SemaphoreType.DMA,
-            pltpu.SemaphoreType.DMA((8,)),
-            pltpu.SemaphoreType.DMA((8,)),
+            pltpu.SemaphoreType.DMA((11,)),
+            pltpu.SemaphoreType.DMA((11,)),
         ],
         compiler_params=pltpu.CompilerParams(collective_id=0, has_side_effects=True),
     )(

time: 45.5 us -> 44.3 us (0.974)
  Pallas kernels: 44.8 us -> 43.6 us
    pallas_call x1, Pallas kernels: 44.8 us -> 43.6 us  [on_device(): pl.pallas_call(kernel, out_shape=pltpu.VMEM(defect.shape, F32), in_specs=...]
where the time goes in v3:
time: 44.3 us; the launch traced here: 44.2 us
  Pallas kernels  43.6 us (98%)
  local copies, waits for them, and re-layouts  0.6 us (1%)
    pallas_call x1, Pallas kernels, on_device(): pl.pallas_call(kernel, out_shape=pltpu.VMEM(defect.shape, F32), in_specs=...  43.6 us

profile of v3, /device:TPU:1, one launch (start us, length us, event | category | flops | bytes accessed | tf_op | source)
XLA Modules:
  0.0 44.2 jit_solution(15905883205565882935)
XLA Ops:
  0.0 43.6 %shard_map.64 = f32[12,128]{1,0:T(8,128)S(1)} custom-call(f32[12,128]{1,0:T(8,128)} %defect_hbm.1, f32[12,128]{1,0:T(8,128)} %mass_hbm.1, f32[12,128,128]{2,1,0:T(8,128)} %diag_hbm.1, f32[96,128,128]{2,1,0:T(8,128)} %coup_hbm.1, s32[1,96]{1,0:T(1,128)} %bitcast.2, s32[1,96]{1,0:T(1,128)} %bitcast.3), custom_call_target="tpu_custom_call" | custom-call | tf_op jit(solution)/shard_map/pallas_call | solution.py:429
  43.6 0.6 %copy.8 = f32[12,128]{1,0:T(8,128)} copy(f32[12,128]{1,0:T(8,128)S(1)} %shard_map.64) | data formatting | bytes 12288

commit v4 on v3

--- a/solution.py
+++ b/solution.py
@@ -19,13 +19,17 @@
 
 
 def distance(offset):
-    return sum(min(step, 4 - step) for step in offset[:3]) + 0.5 * offset[3]
+    return sum(min(step, 4 - step) for step in offset[:3])
+
+
+def mixed(offset):
+    at = offset[0] * 32 + offset[1] * 8 + offset[2] * 2 + offset[3]
+    return at * 37 % 128
 
 
 OFFSETS = sorted(
     (o for o in itertools.product(range(4), range(4), range(4), range(2)) if any(o)),
-    key=distance,
-    reverse=True,
+    key=lambda o: (-distance(o), mixed(o)),
 )
 
 
@@ -348,13 +352,13 @@
 
     u_high, u_low = halves(u0)
     push(u_high, u_low, 0)
-    send_push(0)
     received(req_in.at[one_row], 0)
     req = req_in[...]
     asked = req[:, 0:1].astype(jnp.int32) - 1
     oh_fetch_out[...] = jnp.where((asked == slot) & (lanes < 48), 1.0, 0.0).astype(BF16)
     make_x(u0, u_high, u_low, None, 0)
     send_x(0)(N)
+    send_push(0)
     landing = req[:, 1:2].astype(jnp.int32) - 1
     into = jnp.where(landing == lanes, 1.0, 0.0).T[0:16].astype(BF16)
     oh_push_in[:, 0:B] = into
@@ -369,7 +373,7 @@
         high, low = halves(vector)
         make_x(vector, high, low, row, at)
         more = send_x(at)
-        push(high, low, at, lambda: more(5))
+        push(high, low, at, lambda: more(6))
         more(N)
         send_push(at)
 
@@ -388,31 +392,12 @@
     row = packed([total(v0 * w2), total(v1 * w2), total(v2 * w2), total(w2 * w2)])
     f_out[...] = jnp.broadcast_to(row, (8, B))
     send(lambda p: f_out.at[0:1], lambda m: f_in.at[m : m + 1], 7)
-    received(f_in.at[one_row], 7)
-    sums = jnp.sum(f_in[...], axis=0, keepdims=True) + row
-    h02, h12, h22, square = unpacked(sums, 4)
-    h32 = jnp.sqrt(square - h02 * h02 - h12 * h12 - h22 * h22)
-
-    h00, h11, h22 = h00 + SHIFT, h11 + SHIFT, h22 + SHIFT
-    g00 = h00 * h00 + h10 * h10
-    g10 = h01 * h00 + h11 * h10
-    g20 = h02 * h00 + h12 * h10
-    g11 = h01 * h01 + h11 * h11 + h21 * h21
-    g21 = h02 * h01 + h12 * h11 + h22 * h21
-    g22 = h02 * h02 + h12 * h12 + h22 * h22 + h32 * h32
-    l00 = jnp.sqrt(g00)
-    l10, l20 = g10 / l00, g20 / l00
-    l11 = jnp.sqrt(g11 - l10 * l10)
-    l21 = (g21 - l20 * l10) / l11
-    l22 = jnp.sqrt(g22 - l20 * l20 - l21 * l21)
-    t0 = beta * h00 / l00
-    t1 = (beta * h01 - l10 * t0) / l11
-    t2 = (beta * h02 - l20 * t0 - l21 * t1) / l22
-    m2 = t2 / l22
-    m1 = (t1 - l21 * m2) / l11
-    m0 = (t0 - l10 * m1 - l20 * m2) / l00
-    update = m0 * v0 + m1 * v1 + m2 * v2
-    out_ref[...] = update[0:RB]
+    h00, h11 = h00 + SHIFT, h11 + SHIFT
+    l00_inv = 1.0 / jnp.sqrt(h00 * h00 + h10 * h10)
+    l10 = (h01 * h00 + h11 * h10) * l00_inv
+    l11_inv = 1.0 / jnp.sqrt(h01 * h01 + h11 * h11 + h21 * h21 - l10 * l10)
+    t0 = beta * h00 * l00_inv
+    t1 = (beta * h01 - l10 * t0) * l11_inv
 
     sent(req_out.at[one_row], 0)
     for at in range(3):
@@ -420,6 +405,20 @@
         sent(xp_in.at[at, planes, rest_rows], 1 + at)
         sent(x_far.at[at, planes, far_rows], 8 + at)
         sent(xp_in.at[at, 2, one_row], 4 + at)
+    received(f_in.at[one_row], 7)
+    sums = jnp.sum(f_in[...], axis=0, keepdims=True) + row
+    h02, h12, h22, square = unpacked(sums, 4)
+    h32_square = square - h02 * h02 - h12 * h12 - h22 * h22
+    h22 = h22 + SHIFT
+    l20 = (h02 * h00 + h12 * h10) * l00_inv
+    l21 = (h02 * h01 + h12 * h11 + h22 * h21 - l20 * l10) * l11_inv
+    pivot = h02 * h02 + h12 * h12 + h22 * h22 + h32_square - l20 * l20 - l21 * l21
+    m2 = (beta * h02 - l20 * t0 - l21 * t1) / pivot
+    m1 = (t1 - l21 * m2) * l11_inv
+    m0 = (t0 - l10 * m1 - l20 * m2) * l00_inv
+    update = m0 * v0 + m1 * v1 + m2 * v2
+    out_ref[...] = update[0:RB]
+
     sent(f_in.at[one_row], 7)
 
 

time: 44.3 us -> 43.9 us (level)
  no operation moved by 1% of the time
where the time goes in v4:
time: 43.9 us; the launch traced here: 43.8 us
  Pallas kernels  43.2 us (98%)
  local copies, waits for them, and re-layouts  0.6 us (1%)
    pallas_call x1, Pallas kernels, on_device(): pl.pallas_call(kernel, out_shape=pltpu.VMEM(defect.shape, F32), in_specs=...  43.2 us

profile of v4, /device:TPU:1, one launch (start us, length us, event | category | flops | bytes accessed | tf_op | source)
XLA Modules:
  0.0 43.8 jit_solution(18262279328164534148)
XLA Ops:
  0.0 43.2 %shard_map.64 = f32[12,128]{1,0:T(8,128)S(1)} custom-call(f32[12,128]{1,0:T(8,128)} %defect_hbm.1, f32[12,128]{1,0:T(8,128)} %mass_hbm.1, f32[12,128,128]{2,1,0:T(8,128)} %diag_hbm.1, f32[96,128,128]{2,1,0:T(8,128)} %coup_hbm.1, s32[1,96]{1,0:T(1,128)} %bitcast.2, s32[1,96]{1,0:T(1,128)} %bitcast.3), custom_call_target="tpu_custom_call" | custom-call | tf_op jit(solution)/shard_map/pallas_call | solution.py:428
  43.2 0.6 %copy.8 = f32[12,128]{1,0:T(8,128)} copy(f32[12,128]{1,0:T(8,128)S(1)} %shard_map.64) | data formatting | bytes 12288

commit v5 on v4

--- a/solution.py
+++ b/solution.py
@@ -293,12 +293,13 @@
 
         return more
 
-    def push(high, low, at, between=lambda: None):
+    def push(high, low, at, between=lambda: None, last=lambda: None):
         picked = dot(oh_cols[...], jnp.concatenate([high, low], axis=1)).astype(BF16)
         for b in range(3):
             products[16 * b : 16 * b + 16] = block_products(
                 picked[16 * b : 16 * b + 16], 8 * b, between
             )
+        last()
         p_high, p_low = halves(products[...])
         xp_out[at, 2] = dot(oh_push_out[...], jnp.concatenate([p_high, p_low], axis=0))
 
@@ -373,8 +374,7 @@
         high, low = halves(vector)
         make_x(vector, high, low, row, at)
         more = send_x(at)
-        push(high, low, at, lambda: more(6))
-        more(N)
+        push(high, low, at, lambda: more(4), lambda: more(N))
         send_push(at)
 
         def reduced():

time: 43.9 us -> 44.1 us (level)
  no operation moved by 1% of the time
where the time goes in v5:
time: 44.1 us; the launch traced here: 44 us
  Pallas kernels  43.4 us (98%)
  local copies, waits for them, and re-layouts  0.6 us (1%)
    pallas_call x1, Pallas kernels, on_device(): pl.pallas_call(kernel, out_shape=pltpu.VMEM(defect.shape, F32), in_specs=...  43.4 us

profile of v5, /device:TPU:1, one launch (start us, length us, event | category | flops | bytes accessed | tf_op | source)
XLA Modules:
  0.0 44.0 jit_solution(136360263683767038)
XLA Ops:
  0.0 43.4 %shard_map.64 = f32[12,128]{1,0:T(8,128)S(1)} custom-call(f32[12,128]{1,0:T(8,128)} %defect_hbm.1, f32[12,128]{1,0:T(8,128)} %mass_hbm.1, f32[12,128,128]{2,1,0:T(8,128)} %diag_hbm.1, f32[96,128,128]{2,1,0:T(8,128)} %coup_hbm.1, s32[1,96]{1,0:T(1,128)} %bitcast.2, s32[1,96]{1,0:T(1,128)} %bitcast.3), custom_call_target="tpu_custom_call" | custom-call | tf_op jit(solution)/shard_map/pallas_call | solution.py:428
  43.4 0.6 %copy.8 = f32[12,128]{1,0:T(8,128)} copy(f32[12,128]{1,0:T(8,128)S(1)} %shard_map.64) | data formatting | bytes 12288

commit v6 on v4

--- a/solution.py
+++ b/solution.py
@@ -107,7 +107,9 @@
     nothing = jnp.zeros((1, B), F32)
     req_in[0:1] = nothing
     f_in[0:1] = nothing
-    xp_in[...] = jnp.zeros_like(xp_in)
+    for at in range(3):
+        xp_in[at, 0:2] = jnp.zeros((2, N, B), F32)
+        xp_in[at, 2, 0:1] = nothing
     x_far[...] = jnp.zeros_like(x_far)
 
     barrier = pltpu.get_barrier_semaphore()
@@ -373,7 +375,8 @@
         high, low = halves(vector)
         make_x(vector, high, low, row, at)
         more = send_x(at)
-        push(high, low, at, lambda: more(6))
+        more(20)
+        push(high, low, at, lambda: more(4))
         more(N)
         send_push(at)
 

time: 43.9 us -> 43.9 us (level)
  no operation moved by 1% of the time
where the time goes in v6:
time: 43.9 us; the launch traced here: 43.8 us
  Pallas kernels  43.2 us (98%)
  local copies, waits for them, and re-layouts  0.6 us (1%)
    pallas_call x1, Pallas kernels, on_device(): pl.pallas_call(kernel, out_shape=pltpu.VMEM(defect.shape, F32), in_specs=...  43.2 us

profile of v6, /device:TPU:1, one launch (start us, length us, event | category | flops | bytes accessed | tf_op | source)
XLA Modules:
  0.0 43.8 jit_solution(2969655957171986083)
XLA Ops:
  0.0 43.2 %shard_map.64 = f32[12,128]{1,0:T(8,128)S(1)} custom-call(f32[12,128]{1,0:T(8,128)} %defect_hbm.1, f32[12,128]{1,0:T(8,128)} %mass_hbm.1, f32[12,128,128]{2,1,0:T(8,128)} %diag_hbm.1, f32[96,128,128]{2,1,0:T(8,128)} %coup_hbm.1, s32[1,96]{1,0:T(1,128)} %bitcast.2, s32[1,96]{1,0:T(1,128)} %bitcast.3), custom_call_target="tpu_custom_call" | custom-call | tf_op jit(solution)/shard_map/pallas_call | solution.py:431
  43.2 0.6 %copy.8 = f32[12,128]{1,0:T(8,128)} copy(f32[12,128]{1,0:T(8,128)S(1)} %shard_map.64) | data formatting | bytes 12288
